TPU v7x, 32 devices: a whole 2x2x4 slice. The times are simulated.
32 devices in a mesh: dp: 8 (over z, x), tensor: 4 (over y, core).
Axes of the slice: x: 2, y: 2, z: 4, core: 2. Of those that a mesh axis runs over, the one named last changes fastest.
Arguments:
- tokens: bfloat16 [16, 128, 2048], P('dp'), may hold values from -6 to 6
- cotangent: bfloat16 [16, 128, 2048], P('dp'), may hold values from -6 to 6
- routes: int32 [16, 128, 4], P('dp'), may hold values from 0 to 5, as said below
- gates: bfloat16 [16, 128, 4], P('dp'), may hold values from 0.099609375 to 0.5
- lengths: int32 [16], P('dp'), may hold values from 64 to 128, as said below
- deal: int32 [16], replicated, may hold values from 0 to 15, as said below
- norm1_gain: float32 [2048], P('dp'), may hold values from 0.1 to 1.9
- q_weight: float32 [2048, 2048], P('dp', 'tensor'), may hold values from -0.125 to 0.125
- q_bias: float32 [16, 128], P('tensor', 'dp'), may hold values from -3 to 3
- k_weight: float32 [2048, 2048], P('dp', 'tensor'), may hold values from -0.125 to 0.125
- v_weight: float32 [2048, 2048], P('dp', 'tensor'), may hold values from -0.125 to 0.125
- v_bias: float32 [16, 128], P('tensor', 'dp'), may hold values from -3 to 3
- o_weight: float32 [2048, 2048], P('tensor', 'dp'), may hold values from -0.75 to 0.75
- norm2_gain: float32 [2048], P('dp'), may hold values from 0.1 to 1.9
- expert_gate: float32 [6, 2048, 1408], P(None, 'dp', 'tensor'), may hold values from -0.125 to 0.125
- expert_up: float32 [6, 2048, 1408], P(None, 'dp', 'tensor'), may hold values from -0.125 to 0.125
- expert_down: float32 [6, 1408, 2048], P(None, 'tensor', 'dp'), may hold values from -0.21875 to 0.21875
- shared_gate: float32 [2048, 5632], P('dp', 'tensor'), may hold values from -0.125 to 0.125
- shared_up: float32 [2048, 5632], P('dp', 'tensor'), may hold values from -0.125 to 0.125
- shared_down: float32 [5632, 2048], P('tensor', 'dp'), may hold values from -0.109375 to 0.109375
- shared_switch: float32 [2048], P('dp'), may hold values from -0.125 to 0.125
Outputs:
- output: float32 [16, 128, 2048], P('dp', None, 'tensor')
- tokens_grad: float32 [16, 128, 2048], P('dp', None, 'tensor')
- norm1_gain_grad: float32 [2048], P('dp')
- q_weight_grad: float32 [2048, 2048], P('dp', 'tensor')
- q_bias_grad: float32 [16, 128], P('tensor', 'dp')
- k_weight_grad: float32 [2048, 2048], P('dp', 'tensor')
- v_weight_grad: float32 [2048, 2048], P('dp', 'tensor')
- v_bias_grad: float32 [16, 128], P('tensor', 'dp')
- o_weight_grad: float32 [2048, 2048], P('tensor', 'dp')
- norm2_gain_grad: float32 [2048], P('dp')
- expert_gate_grad: float32 [6, 2048, 1408], P(None, 'dp', 'tensor')
- expert_up_grad: float32 [6, 2048, 1408], P(None, 'dp', 'tensor')
- expert_down_grad: float32 [6, 1408, 2048], P(None, 'tensor', 'dp')
- shared_gate_grad: float32 [2048, 5632], P('dp', 'tensor')
- shared_up_grad: float32 [2048, 5632], P('dp', 'tensor')
- shared_down_grad: float32 [5632, 2048], P('tensor', 'dp')
- shared_switch_grad: float32 [2048], P('dp')
Inputs may be any that keep to these rules, and one draw needn't show every extreme that they name: Sequences 2i and 2i+1 are given on dp index i. The two sequences dealt to one dp index have lengths adding up to exactly 192. `deal`: dealt slot 2i holds sequence 2i; the odd sequences move by one common rotation of the dp indices: slot 2i+1 holds sequence 2((i - r) mod the number of dp indices) + 1, for one r of the draw. `routes`: each row names 4 different experts. Among the 192 real tokens dealt to one dp index, every expert is named by exactly 128 tokens. Rows past a sequence's length hold valid ids too.
All inputs are finite; a program needn't handle non-finite values.
Results may differ from a plain program's by a relative error of at most 0.013.
The roundings to bfloat16 on the way count: a program that leaves them out, or rounds other values in their place, can miss the bound.
Values may be sent and summed in bfloat16 or wider, within the bound.
A program may use at most 256 MiB of HBM per device.

v0:
```python
from functools import partial
import jax
import jax.numpy as jnp
from jax import lax
from jax.sharding import PartitionSpec as P

HEAD_DIM = 128
EPSILON = 1e-06
NEGATIVE = -1e30
LANES = 128
BF16 = jnp.bfloat16
F32 = jnp.float32
ALL = ("dp", "tensor")


def normalize(values, gain):
    return values * lax.rsqrt(jnp.mean(values * values, axis=-1, keepdims=True) + EPSILON) * gain


def nt(left, right):
    return lax.dot_general(left, right, (((1,), (1,)), ((), ())), preferred_element_type=F32)


def tn(left, right):
    return lax.dot_general(left, right, (((0,), (0,)), ((), ())), preferred_element_type=F32)


def nn(left, right):
    return lax.dot_general(left, right, (((1,), (0,)), ((), ())), preferred_element_type=F32)


def gather_all(value):
    return lax.all_gather(value, ALL, axis=0, tiled=True)


def scatter_all(value):
    return lax.psum_scatter(value, ALL, scatter_dimension=0, tiled=True)


def exchange_dp(value):
    return lax.all_to_all(value, "dp", 0, 0, tiled=False)


def per_device(
    tokens,
    cotangent,
    routes,
    gates,
    lengths,
    deal,
    norm1_gain,
    q_weight,
    q_bias,
    k_weight,
    v_weight,
    v_bias,
    o_weight,
    norm2_gain,
    expert_gate,
    expert_up,
    expert_down,
    shared_gate,
    shared_up,
    shared_down,
    shared_switch,
):
    n_dp = lax.axis_size("dp")
    n_tensor = lax.axis_size("tensor")
    place = lax.axis_index("dp")
    member = lax.axis_index("tensor")
    seqs, span, width = tokens.shape
    rows = seqs * span
    shard = rows // n_tensor
    experts, slice_d, expert_cols = expert_gate.shape
    shared_cols = shared_gate.shape[1]
    head_cols = q_weight.shape[1]
    heads = head_cols // HEAD_DIM

    def own_rows(value):
        return lax.dynamic_slice_in_dim(value, member * shard, shard, 0)

    valid = (jnp.arange(span)[None, :] < lengths[:, None]).reshape(rows, 1)
    dense = jnp.zeros((seqs, span, LANES), F32)
    for rank in range(routes.shape[-1]):
        hit = routes[..., rank, None] == jnp.arange(LANES)
        dense = dense + jnp.where(hit, gates[..., rank, None].astype(F32), 0.0)
    dense = dense.reshape(rows, LANES).astype(BF16)
    cot = jnp.where(valid, cotangent.reshape(rows, width), 0).astype(BF16)
    cot_packed = gather_all(own_rows(jnp.concatenate([cot, dense], axis=1)))
    small = jnp.concatenate(
        [norm1_gain, norm2_gain, shared_switch, q_bias.reshape(-1), v_bias.reshape(-1)]
    ).astype(BF16)
    small = lax.all_gather(small[None, :], "dp", axis=0, tiled=True)
    gain_one = small[:, :slice_d].reshape(-1).astype(F32)
    gain_two = small[:, slice_d : 2 * slice_d].reshape(-1).astype(F32)
    switch = small[:, 2 * slice_d : 3 * slice_d].reshape(1, -1)
    piece = q_bias.shape[1]

    def whole_bias(start):
        part = small[:, start : start + heads * piece].reshape(n_dp, heads, piece)
        return part.transpose(1, 0, 2).reshape(-1).astype(F32)

    bias_q = whole_bias(3 * slice_d)
    bias_v = whole_bias(3 * slice_d + heads * piece)
    attn_weights = jnp.concatenate(
        [
            q_weight.astype(BF16),
            k_weight.astype(BF16),
            v_weight.astype(BF16),
            o_weight.T.astype(BF16),
        ],
        axis=1,
    )
    attn_weights = lax.all_gather(attn_weights, "dp", axis=0, tiled=True)
    weight_qkv = attn_weights[:, : 3 * head_cols]
    weight_o = attn_weights[:, 3 * head_cols :]

    def by_unit(expert_part, shared_part):
        return jnp.concatenate(
            [
                expert_part.astype(BF16).reshape(n_dp, -1, slice_d),
                shared_part.astype(BF16).reshape(n_dp, -1, slice_d),
            ],
            axis=1,
        )

    gate_sent = by_unit(
        expert_gate.astype(BF16).transpose(0, 2, 1).reshape(-1, slice_d), shared_gate.astype(BF16).T
    )
    up_sent = by_unit(
        expert_up.astype(BF16).transpose(0, 2, 1).reshape(-1, slice_d), shared_up.astype(BF16).T
    )
    down_sent = by_unit(expert_down.reshape(-1, slice_d), shared_down)
    arrived = exchange_dp(jnp.stack([gate_sent, up_sent, down_sent], axis=1))
    units = arrived.shape[2]
    routed = experts * expert_cols // n_dp
    arrived = arrived.transpose(1, 2, 0, 3).reshape(3, units, width)
    gate_units, up_units, down_units = (arrived[0], arrived[1], arrived[2])
    inputs = tokens.reshape(rows, width).astype(F32)
    inputs_own = own_rows(inputs)
    normed_one = normalize(inputs, gain_one).astype(BF16)
    projected = nn(normed_one, weight_qkv)
    head_shape = (seqs, span, heads, HEAD_DIM)
    queries = (projected[:, :head_cols] + bias_q).astype(BF16).reshape(head_shape)
    keys = projected[:, head_cols : 2 * head_cols].astype(BF16).reshape(head_shape)
    values = (projected[:, 2 * head_cols :] + bias_v).astype(BF16).reshape(head_shape)
    order = jnp.arange(span)
    causal = order[None, :] <= order[:, None]
    scale = HEAD_DIM ** (-0.5)
    scores = jnp.einsum("bqhd,bkhd->bhqk", queries, keys, preferred_element_type=F32) * scale
    scores = jnp.where(causal, scores, NEGATIVE)
    top = jnp.max(scores, axis=-1, keepdims=True)
    powers = jnp.exp(scores - top)
    probs = powers / jnp.sum(powers, axis=-1, keepdims=True)
    probs_low = probs.astype(BF16)
    attended = (
        jnp.einsum("bhqk,bkhd->bqhd", probs_low, values, preferred_element_type=F32)
        .reshape(rows, -1)
        .astype(BF16)
    )
    attn_part = nt(attended, weight_o)
    middle = inputs_own + lax.psum_scatter(attn_part, "tensor", scatter_dimension=0, tiled=True)
    normed_two = gather_all(normalize(middle, gain_two).astype(BF16))
    cot_all = cot_packed[:, :width]
    route_share = cot_packed[:, width : width + LANES]
    unit_expert = (place * routed + jnp.arange(routed)) // expert_cols
    picks = (jnp.arange(LANES)[:, None] == unit_expert[None, :]).astype(BF16)
    gate_logit = nt(normed_two, switch)
    switch_gate = jax.nn.sigmoid(gate_logit)
    share = jnp.concatenate(
        [
            nn(route_share, picks),
            jnp.broadcast_to(switch_gate, (switch_gate.shape[0], units - routed)),
        ],
        axis=1,
    )
    gate_act = nt(normed_two, gate_units)
    up_act = nt(normed_two, up_units)
    logistic = jax.nn.sigmoid(gate_act)
    silu = gate_act * logistic
    inner = (silu * up_act).astype(BF16).astype(F32)
    inner_share = (inner * share).astype(BF16)
    mixed = nn(inner_share, down_units).astype(BF16)
    mixed = lax.psum_scatter(mixed, "dp", scatter_dimension=0, tiled=True)
    mixed = lax.psum_scatter(mixed, "tensor", scatter_dimension=1, tiled=True)
    grad_inner_raw = nt(cot_all, down_units)
    grad_logit = (
        jnp.sum(inner[:, routed:] * grad_inner_raw[:, routed:], axis=1, keepdims=True)
        * switch_gate
        * (1.0 - switch_gate)
    )
    grad_inner = grad_inner_raw * share
    slope = logistic * (1.0 + gate_act * (1.0 - logistic))
    grad_gate_act = (grad_inner * up_act * slope).astype(BF16)
    grad_up_act = (grad_inner * silu).astype(BF16)
    back_two = nn(grad_gate_act, gate_units) + nn(grad_up_act, up_units)
    back_two = (back_two + grad_logit * switch.astype(F32)).astype(BF16)
    back_two = scatter_all(back_two).astype(F32)
    grad_down = tn(inner_share, cot_all)
    grad_gate = tn(grad_gate_act, normed_two)
    grad_up = tn(grad_up_act, normed_two)
    grad_switch = jnp.sum(grad_logit * normed_two.astype(F32), axis=0)
    sent_back = jnp.stack([grad_gate, grad_up, grad_down]).astype(BF16)
    sent_back = sent_back.reshape(3, units, n_dp, slice_d).transpose(2, 0, 1, 3)
    returned = exchange_dp(sent_back).astype(F32)

    def split_units(value):
        routed_part = value[:, :routed].reshape(experts, expert_cols, slice_d)
        return (routed_part, value[:, routed:].reshape(shared_cols, slice_d))

    grad_gate_experts, grad_gate_shared = split_units(returned[:, 0])
    grad_up_experts, grad_up_shared = split_units(returned[:, 1])
    grad_down_experts, grad_down_shared = split_units(returned[:, 2])
    unused_two, norm_two_back = jax.vjp(normalize, middle, gain_two)
    grad_middle_norm, grad_gain_two = norm_two_back(back_two)
    grad_middle = own_rows(cot).astype(F32) + grad_middle_norm
    grad_attn = lax.all_gather(grad_middle.astype(BF16), "tensor", axis=0, tiled=True)
    grad_weight_o = tn(grad_attn, attended)
    grad_attended = nn(grad_attn, weight_o).astype(BF16).reshape(head_shape)
    grad_values = (
        jnp.einsum("bhqk,bqhd->bkhd", probs_low, grad_attended, preferred_element_type=F32)
        .astype(BF16)
        .reshape(rows, -1)
    )
    grad_probs = jnp.einsum("bqhd,bkhd->bhqk", grad_attended, values, preferred_element_type=F32)
    grad_scores = (
        probs * (grad_probs - jnp.sum(grad_probs * probs, axis=-1, keepdims=True))
    ).astype(BF16)
    grad_queries = (
        (jnp.einsum("bhqk,bkhd->bqhd", grad_scores, keys, preferred_element_type=F32) * scale)
        .astype(BF16)
        .reshape(rows, -1)
    )
    grad_keys = (
        (jnp.einsum("bhqk,bqhd->bkhd", grad_scores, queries, preferred_element_type=F32) * scale)
        .astype(BF16)
        .reshape(rows, -1)
    )
    grad_qkv = jnp.concatenate([grad_queries, grad_keys, grad_values], axis=1)
    grad_attn_weights = jnp.concatenate([tn(normed_one, grad_qkv), grad_weight_o], axis=1).astype(
        BF16
    )
    grad_attn_weights = lax.psum_scatter(
        grad_attn_weights, "dp", scatter_dimension=0, tiled=True
    ).astype(F32)
    back_one = nt(grad_qkv, weight_qkv)
    back_one = lax.psum_scatter(back_one, "tensor", scatter_dimension=0, tiled=True)
    unused_one, norm_one_back = jax.vjp(normalize, inputs_own, gain_one)
    grad_input_norm, grad_gain_one = norm_one_back(back_one)
    grad_input = grad_middle + grad_input_norm
    bias_part = jnp.concatenate(
        [
            jnp.sum(grad_queries.astype(F32), axis=0).reshape(heads, n_dp, piece),
            jnp.sum(grad_values.astype(F32), axis=0).reshape(heads, n_dp, piece),
        ],
        axis=0,
    )
    bias_part = bias_part.transpose(1, 0, 2).reshape(1, n_dp, -1)
    mine = (jnp.arange(n_tensor) == member)[:, None, None]
    bias_part = jnp.where(mine, bias_part, 0.0)
    gains = jnp.concatenate([grad_gain_one, grad_gain_two, grad_switch])
    gains = gains.reshape(1, 3, n_dp, slice_d).transpose(0, 2, 1, 3).reshape(n_dp, 3 * slice_d)
    pack = jnp.concatenate([gains, bias_part.transpose(1, 0, 2).reshape(n_dp, -1)], axis=1)
    pack = lax.psum(pack, ALL)
    pack = lax.dynamic_slice_in_dim(pack, place, 1, 0)[0]
    bias_own = lax.dynamic_slice_in_dim(
        pack[3 * slice_d :].reshape(n_tensor, 2, heads, piece), member, 1, 0
    )[0]

    def to_columns(value):
        return lax.all_to_all(value, "tensor", 1, 0, tiled=True)

    out_shape = (seqs, span, width // n_tensor)
    output = jnp.where(valid, to_columns(middle) + mixed.astype(F32), 0.0).reshape(out_shape)
    tokens_grad = jnp.where(valid, to_columns(grad_input), 0.0).reshape(out_shape)
    return (
        output,
        tokens_grad,
        pack[:slice_d],
        grad_attn_weights[:, :head_cols],
        bias_own[0],
        grad_attn_weights[:, head_cols : 2 * head_cols],
        grad_attn_weights[:, 2 * head_cols : 3 * head_cols],
        bias_own[1],
        grad_attn_weights[:, 3 * head_cols :].T,
        pack[slice_d : 2 * slice_d],
        grad_gate_experts.transpose(0, 2, 1),
        grad_up_experts.transpose(0, 2, 1),
        grad_down_experts,
        grad_gate_shared.T,
        grad_up_shared.T,
        grad_down_shared,
        pack[2 * slice_d : 3 * slice_d],
    )


IN_SPECS = (
    P("dp", None, None),
    P("dp", None, None),
    P("dp", None, None),
    P("dp", None, None),
    P("dp"),
    P(),
    P("dp"),
    P("dp", "tensor"),
    P("tensor", "dp"),
    P("dp", "tensor"),
    P("dp", "tensor"),
    P("tensor", "dp"),
    P("tensor", "dp"),
    P("dp"),
    P(None, "dp", "tensor"),
    P(None, "dp", "tensor"),
    P(None, "tensor", "dp"),
    P("dp", "tensor"),
    P("dp", "tensor"),
    P("tensor", "dp"),
    P("dp"),
)
OUT_SPECS = (P("dp", None, "tensor"), P("dp", None, "tensor")) + IN_SPECS[6:]


def solution(mesh):
    return jax.shard_map(
        per_device, mesh=mesh, in_specs=IN_SPECS, out_specs=OUT_SPECS, check_vma=False
    )
```

profile of v0, /device:TPU:0, one launch (start us, length us, event | category | flops | bytes accessed | tf_op | source)
XLA Modules:
  0.0 1104.9 jit_solution(10503144483082694511)
XLA Ops:
  13.3 33.5 %all-gather = bf16[8,1,896]{2,1,0:T(2,128)(2,1)S(1)} all-gather(bf16[1,1,896]{2,1,0:T(2,128)(2,1)S(1)} %bitcast.258), channel_id=1, replica_groups=mesh['dp'=8,'tensor'=4] {'dp'}, dimensions={0}, use_global_device_ids=true | all-gather | bytes 16128 | tf_op jit(solution)/shard_map/all_gather | solution.py:93
  49.2 91.7 %all-gather.6.cloned.1.call-done = bf16[2048,2048]{0,1:T(8,128)(2,1)} async-done(((bf16[256,2048]{0,1:T(8,128)(2,1)}), bf16[2048,2048]{0,1:T(8,128)(2,1)}) %all-gather.6.cloned.1.call-update) | async-done | bytes 8388624 | tf_op jit(solution)/shard_map/all_gather | solution.py:114
  140.9 4.6 fusion.7
  156.4 26.3 %reduce-scatter.7.cloned.1.call-done = f32[64,2048]{1,0:T(8,128)} async-done(((f32[256,2048]{1,0:T(8,128)}), f32[64,2048]{1,0:T(8,128)}) %reduce-scatter.7.cloned.1.call-update) | async-done | bytes 524304 | tf_op jit(solution)/shard_map/reduce_scatter | solution.py:162
  200.5 5.5 all-to-all-start.1
  206.3 145.4 %all-to-all-done.1 = bf16[8,3,440,256]{3,2,1,0:T(8,128)(2,1)} async-done(((bf16[8,3,440,256]{3,2,1,0:T(8,128)(2,1)}), bf16[8,3,440,256]{3,2,1,0:T(8,128)(2,1)}, u32[]{:S(2)}, u32[]{:S(2)}) %all-to-all-start.1) | async-done | bytes 5406752 | tf_op jit(solution)/shard_map/all_to_all | solution.py:41
  361.9 44.5 %all-gather.8.cloned.1.call-done = bf16[2048,2048]{1,0:T(8,128)(2,1)} async-done(((bf16[64,2048]{1,0:T(8,128)(2,1)}), bf16[2048,2048]{1,0:T(8,128)(2,1)}) %all-gather.8.cloned.1.call-update) | async-done | bytes 8388624 | tf_op jit(solution)/shard_map/all_gather | solution.py:33
  406.4 5.8 fusion.73
  412.6 5.7 fusion.72
  418.3 5.8 fusion.71
  424.3 11.5 %multiply_convert_fusion = (bf16[2048,440]{0,1:T(8,128)(2,1)}, bf16[2048,440]{0,1:T(8,128)(2,1)S(1)}, bf16[2048,440]{0,1:T(8,128)(2,1)}, f32[2048,440]{0,1:T(8,128)}, f32[2048,440]{0,1:T(8,128)}) fusion(f32[2048,176]{0,1:T(8,128)S(1)} %broadcast_in_dim.169, f32[2048,264]{0,1:T(8,128)S(1)} %copy-done.11, f32[2048,440]{0,1:T(8,128)} %fusion.71, ...), kind=kOutput, calls=%fused_computation.24 | convolution fusion | flops 3709009920 | bytes 33619968 | tf_op jit(solution)/shard_map/dot_general | solution.py:21
  438.5 8.2 fusion.74
  446.6 11.2 %add_convert_fusion = bf16[2048,2048]{1,0:T(8,128)(2,1)} fusion(f32[2048,2048]{1,0:T(8,128)} %fusion.74, f32[2048]{0:T(1024)S(1)} %convert_element_type.270, f32[2048]{0:T(1024)S(1)} %subtract_multiply_fusion, bf16[2048,440]{0,1:T(8,128)(2,1)} %get-tuple-element.98, bf16[440,2048]{1,0:T(8,128)(2,1)S(1)} %bitcast.231), kind=kOutput, calls=%fused_computation.2 | convolution fusion | flops 3707764736 | bytes 28786688 | tf_op jit(solution)/shard_map/dot_general | solution.py:29
  458.4 9.9 convolution_convert_fusion.1
  468.3 138.6 %reduce-scatter.13.cloned.1.call-done = bf16[64,2048]{1,0:T(8,128)(2,1)} async-done(((bf16[2048,2048]{1,0:T(8,128)(2,1)}), bf16[64,2048]{1,0:T(8,128)(2,1)}) %reduce-scatter.13.cloned.1.call-update) | async-done | bytes 262160 | tf_op jit(solution)/shard_map/reduce_scatter | solution.py:37
  610.1 143.7 %reduce-scatter.9.cloned.1.call-done = bf16[256,2048]{1,0:T(8,128)(2,1)} async-done(((bf16[2048,2048]{1,0:T(8,128)(2,1)}), bf16[256,2048]{1,0:T(8,128)(2,1)}) %reduce-scatter.9.cloned.1.call-update) | async-done | bytes 1048592 | tf_op jit(solution)/shard_map/reduce_scatter | solution.py:184
  767.8 6.2 fusion.5
  782.2 8.4 pad_maximum_fusion
  790.6 7.8 fusion.13
  800.8 7.5 convolution_convert_fusion.4
  818.3 4.9 all-to-all-start.3
  824.1 5.1 multiply_reduce_fusion
  829.2 179.2 %all-to-all-done.3 = bf16[8,3,440,256]{3,2,1,0:T(8,128)(2,1)} async-done(((bf16[8,3,440,256]{3,2,1,0:T(8,128)(2,1)}), bf16[8,3,440,256]{3,2,1,0:T(8,128)(2,1)}, u32[]{:S(2)}, u32[]{:S(2)}) %all-to-all-start.3) | async-done | bytes 5406752 | tf_op jit(solution)/shard_map/all_to_all | solution.py:41
  1048.2 41.3 %psum.7 = f32[8,1280]{1,0:T(8,128)S(1)} all-reduce(f32[8,1280]{1,0:T(8,128)S(1)} %pad_maximum_fusion.4), channel_id=1, replica_groups=mesh['dp'=8,'tensor'=4] {'dp','tensor'}, use_global_device_ids=true, to_apply=%region_19.20 | all-reduce | flops 10240 | bytes 81920 | tf_op jit(solution)/shard_map/psum | solution.py:264
  (252 shorter events, 135.7 us)
Async XLA Ops:
  8.0 132.9 %all-gather.6.cloned.1.call-start = ((), (), s32[]{:S(2)}) async-start(), calls=%async_computation.10 | async-start | bytes 9437184 | tf_op jit(solution)/shard_map/all_gather | solution.py:114
  11.7 35.6 %copy-start.4 = (bf16[2,128,2048]{2,1,0:T(8,128)(2,1)S(1)}, bf16[2,128,2048]{2,1,0:T(8,128)(2,1)}, u32[]{:S(2)}) copy-start(bf16[2,128,2048]{2,1,0:T(8,128)(2,1)} %param.21) | copy-start | bytes 3145732
  12.8 169.9 %reduce-scatter.7.cloned.1.call-start = ((), (), s32[]{:S(2)}) async-start(), calls=%async_computation.11 | async-start | bytes 2621440 | tf_op jit(solution)/shard_map/reduce_scatter | solution.py:162
  153.2 205.8 %all-gather.10.cloned.1.call-start = ((), (), s32[]{:S(2)}) async-start(), calls=%async_computation.13 | async-start | bytes 9191424 | tf_op jit(solution)/shard_map/all_gather | solution.py:33
  153.8 28.9 %copy-start.27 = (pred[256]{0:T(512)(128)(4,1)}, pred[256]{0:T(512)(128)(4,1)S(1)}, u32[]{:S(2)}) copy-start(pred[256]{0:T(512)(128)(4,1)S(1)} %get-tuple-element.131) | copy-start | bytes 772
  156.4 250.0 %all-gather.8.cloned.1.call-start = ((), (), s32[]{:S(2)}) async-start(), calls=%async_computation.12 | async-start | bytes 8650752 | tf_op jit(solution)/shard_map/all_gather | solution.py:33
  200.5 151.3 %all-to-all-start.1 = ((bf16[8,3,440,256]{3,2,1,0:T(8,128)(2,1)}), bf16[8,3,440,256]{3,2,1,0:T(8,128)(2,1)}, u32[]{:S(2)}, u32[]{:S(2)}) async-start(bf16[8,3,440,256]{3,2,1,0:T(8,128)(2,1)} %pad_maximum_fusion.1), calls=%async_computation.2 | async-start | bytes 10813440 | tf_op jit(solution)/shard_map/all_to_all | solution.py:41
  206.0 400.9 %reduce-scatter.13.cloned.1.call-start = ((), (), s32[]{:S(2)}) async-start(), calls=%async_computation.16 | async-start | bytes 8650752 | tf_op jit(solution)/shard_map/reduce_scatter | solution.py:37
  406.4 6.3 copy-start.15
  418.3 6.0 copy-start.11
  418.3 6.0 copy-start.14
  435.8 10.8 copy-start.37
  457.9 295.8 %reduce-scatter.9.cloned.1.call-start = ((), (), s32[]{:S(2)}) async-start(), calls=%async_computation.14 | async-start | bytes 9437184 | tf_op jit(solution)/shard_map/reduce_scatter | solution.py:184
  468.3 285.6 %all-gather.12.cloned.1.call-start = ((), (), s32[]{:S(2)}) async-start(), calls=%async_computation.17 | async-start | bytes 1310720 | tf_op jit(solution)/shard_map/all_gather | solution.py:217
  610.0 428.9 %reduce-scatter.11.cloned.1.call-start = ((), (), s32[]{:S(2)}) async-start(), calls=%async_computation.15 | async-start | bytes 1310720 | tf_op jit(solution)/shard_map/reduce_scatter | solution.py:185
  753.8 287.0 %reduce-scatter.15.cloned.1.call-start = ((), (), s32[]{:S(2)}) async-start(), calls=%async_computation.18 | async-start | bytes 2621440 | tf_op jit(solution)/shard_map/reduce_scatter | solution.py:247
  774.0 317.8 %reduce-scatter.17.cloned.1.call-start = ((), (), s32[]{:S(2)}) async-start(), calls=%async_computation.19 | async-start | bytes 9437184 | tf_op jit(solution)/shard_map/reduce_scatter | solution.py:243
  798.4 10.8 slice-start
  800.8 8.4 slice-start.1
  818.3 190.1 %all-to-all-start.3 = ((bf16[8,3,440,256]{3,2,1,0:T(8,128)(2,1)}), bf16[8,3,440,256]{3,2,1,0:T(8,128)(2,1)}, u32[]{:S(2)}, u32[]{:S(2)}) async-start(bf16[8,3,440,256]{3,2,1,0:T(8,128)(2,1)} %maximum_bitcast_fusion), calls=%async_computation.9 | async-start | bytes 10813440 | tf_op jit(solution)/shard_map/all_to_all | solution.py:41
  1008.4 30.5 %all-to-all-start = ((f32[64,4,512]{2,0,1:T(8,128)}), f32[64,4,512]{2,0,1:T(8,128)S(1)}, u32[]{:S(2)}, u32[]{:S(2)}) async-start(f32[64,4,512]{2,0,1:T(8,128)} %bitcast.197), calls=%async_computation.1 | async-start | bytes 1048576 | tf_op jit(solution)/shard_map/all_to_all | solution.py:271
  1035.6 6.7 copy-start.7
  1042.3 48.6 %copy-start.32 = (pred[2,128]{1,0:T(4,128)(4,1)S(1)}, pred[2,128]{1,0:T(4,128)(4,1)}, u32[]{:S(2)}) copy-start(pred[2,128]{1,0:T(4,128)(4,1)} %get-tuple-element.130) | copy-start | bytes 772
  1044.7 46.2 %all-to-all-start.2 = ((f32[64,4,512]{2,0,1:T(8,128)}), f32[64,4,512]{2,0,1:T(8,128)S(1)}, u32[]{:S(2)}, u32[]{:S(2)}) async-start(f32[64,4,512]{2,0,1:T(8,128)} %bitcast.196), calls=%async_computation.7 | async-start | bytes 1048576 | tf_op jit(solution)/shard_map/all_to_all | solution.py:271
  (32 other events, 89.4 us)
Sparse Core Ops, SparseCore 0:
  13.0 127.8 all-gather.5
  153.3 29.3 reduce-scatter.6
  610.1 12.5 all-gather.11
  753.9 23.8 reduce-scatter.10
  780.2 31.1 reduce-scatter.14
  814.9 251.4 reduce-scatter.16
Sparse Core Ops, SparseCore 1:
  157.1 113.9 all-gather.9
  274.4 131.9 all-gather.7
  458.0 148.8 reduce-scatter.12
  610.5 143.2 reduce-scatter.8
where the time goes:
time: 1110 us; the launch traced here: 1100 us
  waiting for transfers between devices  770 us (69%)
  matrix products  111 us (10%)
  blocking collectives  74.8 us (7%)
  local copies, waits for them, and re-layouts  66.3 us (6%)
  other arithmetic  47.6 us (4%)
  starting transfers between devices  18.5 us (2%)
  between operations  16.9 us (2%)
    all_to_all x2, waiting for transfers between devices, exchange_dp(): return lax.all_to_all(value, 'dp', 0, 0, tiled=False)  325 us
    reduce_scatter x1, waiting for transfers between devices, per_device(): mixed = lax.psum_scatter(mixed, 'dp', scatter_dimension=0, tiled=True)  144 us
    reduce_scatter x1, waiting for transfers between devices, scatter_all(): return lax.psum_scatter(value, ALL, scatter_dimension=0, tiled=True)  139 us
    all_gather x1, waiting for transfers between devices, per_device(): attn_weights = lax.all_gather(attn_weights, 'dp', axis=0, tiled=True)  91.7 us
    all_gather x2, waiting for transfers between devices, gather_all(): return lax.all_gather(value, ALL, axis=0, tiled=True)  44.5 us
    psum x1, blocking collectives, per_device(): pack = lax.psum(pack, ALL)  41.3 us
    dot_general x6, matrix products, nn(): lax.dot_general(left, right, (((1,), (0,)), ((), ())), preferred_element_...  40.1 us
    dot_general x6, matrix products, nt(): lax.dot_general(left, right, (((1,), (1,)), ((), ())), preferred_element_...  38.7 us
  transfers between devices with their start and end apart: 14, of which 7 were waited for; matrix products, arithmetic and copies ran while one was open for 13% of the time, Pallas kernels for 0%

commit v1 on v0

--- a/solution.py
+++ b/solution.py
@@ -261,7 +261,7 @@
     gains = jnp.concatenate([grad_gain_one, grad_gain_two, grad_switch])
     gains = gains.reshape(1, 3, n_dp, slice_d).transpose(0, 2, 1, 3).reshape(n_dp, 3 * slice_d)
     pack = jnp.concatenate([gains, bias_part.transpose(1, 0, 2).reshape(n_dp, -1)], axis=1)
-    pack = lax.psum(pack, ALL)
+    pack = jnp.sum(lax.all_gather(pack, ALL), axis=0)
     pack = lax.dynamic_slice_in_dim(pack, place, 1, 0)[0]
     bias_own = lax.dynamic_slice_in_dim(
         pack[3 * slice_d :].reshape(n_tensor, 2, heads, piece), member, 1, 0

time: 1110 us -> 1100 us (level)
  blocking collectives: 74.8 us -> 33.5 us
  waiting for transfers between devices: 770 us -> 808 us
  local copies, waits for them, and re-layouts: 66.3 us -> 50.7 us
    psum x1 -> x0, blocking collectives: 41.3 us -> none  [per_device(): pack = lax.psum(pack, ALL)]
    reduce_scatter x1, waiting for transfers between devices: 0.01 us -> 27.8 us  [per_device(): lax.psum_scatter(back_one, 'tensor', scatter_dimension=0, tiled=True)]
    unnamed x107 -> x131, local copies, waits for them, and re-layouts: 35 us -> 28.1 us
  transfers between devices with their start and end apart: 14 -> 15, of which waited for: 7 -> 10; matrix products, arithmetic and copies ran while one was open for 13% -> 12% of each run, Pallas kernels for 0% -> 0%
where the time goes in v1:
time: 1100 us; the launch traced here: 1090 us
  waiting for transfers between devices  808 us (73%)
  matrix products  107 us (10%)
  other arithmetic  52.7 us (5%)
  local copies, waits for them, and re-layouts  50.7 us (5%)
  blocking collectives  33.5 us (3%)
  starting transfers between devices  20 us (2%)
  between operations  17.3 us (2%)
    all_to_all x2, waiting for transfers between devices, exchange_dp(): return lax.all_to_all(value, 'dp', 0, 0, tiled=False)  322 us
    reduce_scatter x1, waiting for transfers between devices, scatter_all(): return lax.psum_scatter(value, ALL, scatter_dimension=0, tiled=True)  149 us
    reduce_scatter x1, waiting for transfers between devices, per_device(): mixed = lax.psum_scatter(mixed, 'dp', scatter_dimension=0, tiled=True)  139 us
    all_gather x1, waiting for transfers between devices, per_device(): attn_weights = lax.all_gather(attn_weights, 'dp', axis=0, tiled=True)  91.1 us
    all_gather x2, waiting for transfers between devices, gather_all(): return lax.all_gather(value, ALL, axis=0, tiled=True)  43.7 us
    dot_general x6, matrix products, nn(): lax.dot_general(left, right, (((1,), (0,)), ((), ())), preferred_element_...  39 us
    dot_general x6, matrix products, nt(): lax.dot_general(left, right, (((1,), (1,)), ((), ())), preferred_element_...  38.5 us
    all_gather x1, blocking collectives, per_device(): small = lax.all_gather(small[None, :], 'dp', axis=0, tiled=True)  33.5 us
  transfers between devices with their start and end apart: 15, of which 10 were waited for; matrix products, arithmetic and copies ran while one was open for 12% of the time, Pallas kernels for 0%

profile of v1, /device:TPU:0, one launch (start us, length us, event | category | flops | bytes accessed | tf_op | source)
XLA Modules:
  0.0 1089.5 jit_solution(3765501444707938096)
XLA Ops:
  13.3 33.5 %all-gather.1 = bf16[8,1,896]{2,1,0:T(2,128)(2,1)S(1)} all-gather(bf16[1,1,896]{2,1,0:T(2,128)(2,1)S(1)} %bitcast.259), channel_id=1, replica_groups=mesh['dp'=8,'tensor'=4] {'dp'}, dimensions={0}, use_global_device_ids=true | all-gather | bytes 16128 | tf_op jit(solution)/shard_map/all_gather | solution.py:93
  49.8 91.1 %all-gather.8.cloned.1.call-done = bf16[2048,2048]{0,1:T(8,128)(2,1)} async-done(((bf16[256,2048]{0,1:T(8,128)(2,1)}), bf16[2048,2048]{0,1:T(8,128)(2,1)}) %all-gather.8.cloned.1.call-update) | async-done | bytes 8388624 | tf_op jit(solution)/shard_map/all_gather | solution.py:114
  153.9 27.2 %reduce-scatter.7.cloned.1.call-done = f32[64,2048]{1,0:T(8,128)} async-done(((f32[256,2048]{1,0:T(8,128)}), f32[64,2048]{1,0:T(8,128)}) %reduce-scatter.7.cloned.1.call-update) | async-done | bytes 524304 | tf_op jit(solution)/shard_map/reduce_scatter | solution.py:162
  196.0 5.7 all-to-all-start.1
  202.6 147.5 %all-to-all-done.1 = bf16[8,3,440,256]{3,2,1,0:T(8,128)(2,1)} async-done(((bf16[8,3,440,256]{3,2,1,0:T(8,128)(2,1)}), bf16[8,3,440,256]{3,2,1,0:T(8,128)(2,1)}, u32[]{:S(2)}, u32[]{:S(2)}) %all-to-all-start.1) | async-done | bytes 5406752 | tf_op jit(solution)/shard_map/all_to_all | solution.py:41
  360.3 43.7 %all-gather.10.cloned.1.call-done = bf16[2048,2048]{1,0:T(8,128)(2,1)} async-done(((bf16[64,2048]{1,0:T(8,128)(2,1)}), bf16[2048,2048]{1,0:T(8,128)(2,1)}) %all-gather.10.cloned.1.call-update) | async-done | bytes 8388624 | tf_op jit(solution)/shard_map/all_gather | solution.py:33
  403.9 5.8 fusion.73
  410.2 5.7 fusion.72
  415.9 5.8 fusion.71
  421.8 11.4 %multiply_convert_fusion = (bf16[2048,440]{0,1:T(8,128)(2,1)}, bf16[2048,440]{0,1:T(8,128)(2,1)}, bf16[2048,440]{0,1:T(8,128)(2,1)}, f32[2048,440]{0,1:T(8,128)S(1)}, f32[2048,440]{0,1:T(8,128)}) fusion(f32[2048,176]{0,1:T(8,128)S(1)} %broadcast_in_dim.169, f32[2048,264]{0,1:T(8,128)S(1)} %copy-done.9, f32[2048,440]{0,1:T(8,128)} %fusion.71, ...), kind=kOutput, calls=%fused_computation.24 | convolution fusion | flops 3709009920 | bytes 33619968 | tf_op jit(solution)/shard_map/dot_general | solution.py:21
  435.2 8.2 fusion.74
  443.3 10.8 add_convert_fusion
  454.2 148.8 %reduce-scatter.13.cloned.1.call-done = bf16[64,2048]{1,0:T(8,128)(2,1)} async-done(((bf16[2048,2048]{1,0:T(8,128)(2,1)}), bf16[64,2048]{1,0:T(8,128)(2,1)}) %reduce-scatter.13.cloned.1.call-update) | async-done | bytes 262160 | tf_op jit(solution)/shard_map/reduce_scatter | solution.py:37
  606.3 10.0 convolution_convert_fusion.1
  624.9 6.2 fusion.5
  631.2 138.6 %reduce-scatter.9.cloned.1.call-done = bf16[256,2048]{1,0:T(8,128)(2,1)} async-done(((bf16[2048,2048]{1,0:T(8,128)(2,1)}), bf16[256,2048]{1,0:T(8,128)(2,1)}) %reduce-scatter.9.cloned.1.call-update) | async-done | bytes 1048592 | tf_op jit(solution)/shard_map/reduce_scatter | solution.py:184
  775.4 27.8 %reduce-scatter.15.cloned.1.call-done = f32[64,2048]{1,0:T(8,128)} async-done(((f32[256,2048]{1,0:T(8,128)}), f32[64,2048]{1,0:T(8,128)}) %reduce-scatter.15.cloned.1.call-update) | async-done | bytes 524304 | tf_op jit(solution)/shard_map/reduce_scatter | solution.py:247
  807.5 6.0 convolution_convert_fusion
  813.5 7.8 pad_maximum_fusion
  822.7 7.3 fusion.13
  832.4 7.4 convolution_convert_fusion.4
  856.9 174.2 %all-to-all-done.3 = bf16[8,3,440,256]{3,2,1,0:T(8,128)(2,1)} async-done(((bf16[8,3,440,256]{3,2,1,0:T(8,128)(2,1)}), bf16[8,3,440,256]{3,2,1,0:T(8,128)(2,1)}, u32[]{:S(2)}, u32[]{:S(2)}) %all-to-all-start.3) | async-done | bytes 5406752 | tf_op jit(solution)/shard_map/all_to_all | solution.py:41
  1034.7 7.7 copy_convert_fusion
  1069.6 6.7 reduce-scatter.17.cloned.1.call-done
  (279 shorter events, 127.6 us)
Async XLA Ops:
  8.0 132.9 %all-gather.8.cloned.1.call-start = ((), (), s32[]{:S(2)}) async-start(), calls=%async_computation.10 | async-start | bytes 9437184 | tf_op jit(solution)/shard_map/all_gather | solution.py:114
  11.7 36.2 %copy-start.4 = (bf16[2,128,2048]{2,1,0:T(8,128)(2,1)S(1)}, bf16[2,128,2048]{2,1,0:T(8,128)(2,1)}, u32[]{:S(2)}) copy-start(bf16[2,128,2048]{2,1,0:T(8,128)(2,1)} %param.21) | copy-start | bytes 3145732
  12.8 168.2 %reduce-scatter.7.cloned.1.call-start = ((), (), s32[]{:S(2)}) async-start(), calls=%async_computation.11 | async-start | bytes 2621440 | tf_op jit(solution)/shard_map/reduce_scatter | solution.py:162
  49.8 95.7 %copy-start.3 = (bf16[256,2048]{1,0:T(8,128)(2,1)}, bf16[256,2048]{1,0:T(8,128)(2,1)S(1)}, u32[]{:S(2)}) copy-start(bf16[256,2048]{1,0:T(8,128)(2,1)S(1)} %get-tuple-element.110) | copy-start | bytes 3145732
  151.6 205.8 %all-gather.12.cloned.1.call-start = ((), (), s32[]{:S(2)}) async-start(), calls=%async_computation.13 | async-start | bytes 9191424 | tf_op jit(solution)/shard_map/all_gather | solution.py:33
  152.2 30.8 %copy-start.33 = (pred[256]{0:T(512)(128)(4,1)}, pred[256]{0:T(512)(128)(4,1)S(1)}, u32[]{:S(2)}) copy-start(pred[256]{0:T(512)(128)(4,1)S(1)} %get-tuple-element.148) | copy-start | bytes 772
  153.0 451.2 %copy-start.2 = (bf16[256,2048]{1,0:T(8,128)(2,1)}, bf16[256,2048]{1,0:T(8,128)(2,1)S(1)}, u32[]{:S(2)}) copy-start(bf16[256,2048]{1,0:T(8,128)(2,1)S(1)} %bitcast_select_fusion) | copy-start | bytes 3145732
  153.8 250.1 %all-gather.10.cloned.1.call-start = ((), (), s32[]{:S(2)}) async-start(), calls=%async_computation.12 | async-start | bytes 8650752 | tf_op jit(solution)/shard_map/all_gather | solution.py:33
  196.0 154.1 %all-to-all-start.1 = ((bf16[8,3,440,256]{3,2,1,0:T(8,128)(2,1)}), bf16[8,3,440,256]{3,2,1,0:T(8,128)(2,1)}, u32[]{:S(2)}, u32[]{:S(2)}) async-start(bf16[8,3,440,256]{3,2,1,0:T(8,128)(2,1)} %pad_maximum_fusion.1), calls=%async_computation.2 | async-start | bytes 10813440 | tf_op jit(solution)/shard_map/all_to_all | solution.py:41
  201.7 401.3 %reduce-scatter.13.cloned.1.call-start = ((), (), s32[]{:S(2)}) async-start(), calls=%async_computation.16 | async-start | bytes 8650752 | tf_op jit(solution)/shard_map/reduce_scatter | solution.py:37
  454.1 148.8 %copy-start.30 = (f32[64]{0:T(128)S(1)}, f32[64]{0:T(128)}, u32[]{:S(2)}) copy-start(f32[64]{0:T(128)} %copy-done.29) | copy-start | bytes 772
  454.1 150.1 %copy-start.41 = (f32[64]{0:T(128)S(1)}, f32[64]{0:T(128)}, u32[]{:S(2)}) copy-start(f32[64]{0:T(128)} %copy-done.40) | copy-start | bytes 772
  454.1 164.7 %all-gather.14.cloned.1.call-start = ((), (), s32[]{:S(2)}) async-start(), calls=%async_computation.17 | async-start | bytes 1310720 | tf_op jit(solution)/shard_map/all_gather | solution.py:217
  604.2 12.1 %copy-start.35 = (f32[64]{0:T(128)}, f32[64]{0:T(128)S(1)}, u32[]{:S(2)}) copy-start(f32[64]{0:T(128)S(1)} %multiply_multiply_fusion.1) | copy-start | bytes 772
  606.1 163.7 %reduce-scatter.9.cloned.1.call-start = ((), (), s32[]{:S(2)}) async-start(), calls=%async_computation.14 | async-start | bytes 9437184 | tf_op jit(solution)/shard_map/reduce_scatter | solution.py:184
  616.4 186.8 %reduce-scatter.15.cloned.1.call-start = ((), (), s32[]{:S(2)}) async-start(), calls=%async_computation.18 | async-start | bytes 2621440 | tf_op jit(solution)/shard_map/reduce_scatter | solution.py:247
  631.1 138.9 %copy-start.39 = (f32[64]{0:T(128)S(1)}, f32[64]{0:T(128)}, u32[]{:S(2)}) copy-start(f32[64]{0:T(128)} %get-tuple-element.122) | copy-start | bytes 772
  631.1 431.8 %reduce-scatter.11.cloned.1.call-start = ((), (), s32[]{:S(2)}) async-start(), calls=%async_computation.15 | async-start | bytes 1310720 | tf_op jit(solution)/shard_map/reduce_scatter | solution.py:185
  769.8 296.9 %all-gather.16.cloned.1.call-start = ((), (), s32[]{:S(2)}) async-start(), calls=%async_computation.20 | async-start | bytes 1351680 | tf_op jit(solution)/shard_map/all_gather | solution.py:264
  805.3 271.0 %reduce-scatter.17.cloned.1.call-start = ((), (), s32[]{:S(2)}) async-start(), calls=%async_computation.19 | async-start | bytes 9437184 | tf_op jit(solution)/shard_map/reduce_scatter | solution.py:243
  830.0 10.8 slice-start
  850.5 180.6 %all-to-all-start.3 = ((bf16[8,3,440,256]{3,2,1,0:T(8,128)(2,1)}), bf16[8,3,440,256]{3,2,1,0:T(8,128)(2,1)}, u32[]{:S(2)}, u32[]{:S(2)}) async-start(bf16[8,3,440,256]{3,2,1,0:T(8,128)(2,1)} %maximum_bitcast_fusion), calls=%async_computation.9 | async-start | bytes 10813440 | tf_op jit(solution)/shard_map/all_to_all | solution.py:41
  1031.1 13.6 %all-to-all-start = ((f32[64,4,512]{2,0,1:T(8,128)}), f32[64,4,512]{2,0,1:T(8,128)S(1)}, u32[]{:S(2)}, u32[]{:S(2)}) async-start(f32[64,4,512]{2,0,1:T(8,128)} %bitcast.199), calls=%async_computation.1 | async-start | bytes 1048576 | tf_op jit(solution)/shard_map/all_to_all | solution.py:271
  1044.7 20.1 %all-to-all-start.2 = ((f32[64,4,512]{2,0,1:T(8,128)}), f32[64,4,512]{2,0,1:T(8,128)}, u32[]{:S(2)}, u32[]{:S(2)}) async-start(f32[64,4,512]{2,0,1:T(8,128)} %bitcast.198), calls=%async_computation.7 | async-start | bytes 1048576 | tf_op jit(solution)/shard_map/all_to_all | solution.py:271
  (45 other events, 179.5 us)
Sparse Core Ops, SparseCore 0:
  13.0 127.8 all-gather.7
  151.7 29.3 reduce-scatter.6
  606.2 12.5 all-gather.13
  622.3 147.4 reduce-scatter.8
  772.8 30.2 reduce-scatter.14
  805.5 24.7 reduce-scatter.10
  833.9 242.2 reduce-scatter.16
Sparse Core Ops, SparseCore 1:
  155.5 114.0 all-gather.11
  272.9 131.0 all-gather.9
  454.2 148.7 reduce-scatter.12
  805.3 89.9 all-gather.15
